TPU v7x, 128 devices: a whole 4x4x4 slice. The times are simulated.
128 devices in a mesh: gz: 128 (over x, y, z, core).
Axes of the slice: x: 4, y: 4, z: 4, core: 2. Of those that a mesh axis runs over, the one named last changes fastest.
Arguments:
- density: float32 [2, 128, 256, 256], P(None, 'gz'), may hold values from 0.02 to 0.8
- kernel_hat: float32 [256, 512, 512], P(None, 'gz'), may hold values from 0.37 to 7, as said below
Outputs:
- potential: float32 [2, 128, 256, 256], P(None, 'gz')
- energies: float32 [2], replicated
Inputs may be any that keep to these rules, and one draw needn't show every extreme that they name: kernel_hat at (a, b, c) equals kernel_hat at ((-a) mod 256, (-b) mod 512, (-c) mod 512).
All inputs are finite; a program needn't handle non-finite values.
Results may differ from a plain program's by a relative error of at most 0.00015.
Values sent between devices are 32-bit elements; how exact they have to be, the bound alone decides.
No kernel may reach another device: no remote copies, remote signals or barrier semaphores. Data moves between devices by JAX's collectives and lax.ppermute only.
A program may use at most 64 MiB of HBM per device.

v0:
```python
import math

import jax
import jax.numpy as jnp
import numpy as np
from jax import lax
from jax.experimental import pallas as pl
from jax.experimental.pallas import tpu as pltpu
from jax.sharding import Mesh
from jax.sharding import PartitionSpec as P


GZ = ("gz_0", "gz_1", "gz_2", "gz_3")
BLOCKS = ("gz_3", "gz_0", "gz_1", "gz_2")
HGRID = 0.35
STENCIL = (0.8, -0.2, 4.0 / 105.0, -1.0 / 280.0)
KAPPA = 0.804
MU_X = 0.2195149727645171
BETA_C = 0.06672455060314922
GAMMA_C = 0.031090690869654894
FZ_CURV = 1.709921
PARAMS_UNPOL = (0.031091, 0.2137, 7.5957, 3.5876, 1.6382, 0.49294)
PARAMS_POL = (0.015545, 0.20548, 14.1189, 6.1977, 3.3662, 0.62517)
PARAMS_STIFF = (0.016887, 0.11125, 10.357, 3.6231, 0.88026, 0.49671)

F32 = jnp.float32
BF16 = jnp.bfloat16
NZ, NY, NX = 128, 256, 256
MZ, MY, MX = 256, 512, 512
ND = 128
HART = 16
OUT_ROWS = 24
BACK_ROWS = 25
PAIR = ND // 2
CELLS = NZ * NY * NX
Z_CHUNK = 32
XC_ROWS = 8
XC_AHEAD = 12
XC_SPREAD = 19
HART_ORDER = (
    "x00", "x01", "x10", "z00", "z01", "z02", "z03", "z10",
    "b00", "z11", "b01", "z12", "o00", "z13", "o01", "b10",
    "b11", "o10", "o11",
)
NORM = 1.0 / (MX * MY * MZ)
VMEM = pl.BlockSpec(memory_space=pltpu.VMEM)
SMEM = pl.BlockSpec(memory_space=pltpu.SMEM)
HBM = pl.BlockSpec(memory_space=pltpu.HBM)


def halves(m):
    m = np.asarray(m, np.float32)
    hi = m.astype(BF16)
    lo = (m - hi.astype(np.float32)).astype(BF16)
    return np.stack([hi, lo])


def device_of(block):
    return (block & (ND // 2 - 1)) * 2 + (block >> 6)


def y_forward():
    y, q = np.arange(NY), device_of(np.arange(ND))
    first = np.where(q < ND // 2, 4 * q + 1, 4 * q)
    rows = []
    for ky in (first, first + 1):
        angle = 2.0 * np.pi * (np.outer(ky, y) % MY) / MY
        paired = (ky == MY // 2)[:, None]
        rows += [np.cos(angle), np.where(paired, 1.0, -np.sin(angle))]
    return halves(np.concatenate(rows, 0))


def split(value):
    hi = value.astype(BF16)
    lo = (value - hi.astype(F32)).astype(BF16)
    return hi, lo


def dot1(a, b):
    return jnp.dot(a, b, preferred_element_type=F32)


def dot3(a_hi, a_lo, b_hi, b_lo):
    return dot1(a_hi, b_hi) + (dot1(a_lo, b_hi) + dot1(a_hi, b_lo))


def put_rows(ref, row, rows, value, count=ND):
    for half in range(value.shape[1] // 128):
        ref[pl.ds(row + half, count, stride=rows), :] = value[
            :, half * 128 : half * 128 + 128
        ]


def get_rows(ref, row, rows):
    return jnp.concatenate(
        [ref[pl.ds(row + half, ND, stride=rows), :] for half in range(2)], axis=1
    )


def iota(shape, dim):
    return lax.broadcasted_iota(jnp.int32, shape, dim)


def slope_parts(n, place=lambda i: i):
    offset = place(iota((n, n), 1)) - place(iota((n, n), 0))
    parts = []
    coefs = halves([c / HGRID for c in STENCIL]).astype(np.float32)
    for part in range(2):
        value = jnp.zeros((n, n), F32)
        for k in range(1, 5):
            c = float(coefs[part, k - 1])
            value = jnp.where(offset == k, c, jnp.where(offset == -k, -c, value))
        parts.append(value.astype(BF16))
    return parts


def parity_matrix(transposed):
    x, place = iota((NX, NX), int(transposed)), iota((NX, NX), 1 - int(transposed))
    return jnp.where(place == (x & 1) * (NX // 2) + (x >> 1), 1.0, 0.0).astype(BF16)


def cos_sin(product):
    turn = product.astype(jnp.int32) & 511
    quarter = (turn + 64) >> 7
    angle = (turn - 128 * quarter).astype(F32) * (2.0 * math.pi / 512.0)
    sq = angle * angle
    s = angle * (
        1.0 + sq * (-1.0 / 6.0 + sq * (1.0 / 120.0 + sq * (-1.0 / 5040.0 + sq * (1.0 / 362880.0))))
    )
    c = 1.0 + sq * (-0.5 + sq * (1.0 / 24.0 + sq * (-1.0 / 720.0 + sq * (1.0 / 40320.0))))
    odd = (quarter & 1) == 1
    c, s = jnp.where(odd, s, c), jnp.where(odd, c, s)
    return (
        jnp.where(((quarter + 1) & 2) == 2, -c, c),
        jnp.where((quarter & 2) == 2, -s, s),
    )


def put_parts(ref, index, rows, cols, value):
    hi, lo = split(value)
    ref[(*index, 0, rows, cols)] = hi
    ref[(*index, 1, rows, cols)] = lo


def put_rotation(ref, index, row, c, s, transposed):
    n, m = c.shape
    top, low = slice(row, row + n), slice(row + n, row + 2 * n)
    put_parts(ref, index, top, slice(0, m), c)
    put_parts(ref, index, low, slice(m, 2 * m), c)
    put_parts(ref, index, top, slice(m, 2 * m), -s if transposed else s)
    put_parts(ref, index, low, slice(0, m), s if transposed else -s)


def float_iota(shape, dim):
    return iota(shape, dim).astype(F32)


def tables_kernel(wx_ref, wz_ref, wzi_ref, wxi_ref, yb_ref, slope_ref, slope_z_ref):
    for parity in range(2):
        shape = (NX // 2, MX // 2)
        x = 2.0 * float_iota(shape, 0) + parity
        put_rotation(wx_ref, (parity,), 0, *cos_sin(x * float_iota(shape, 1)), True)
        shape = (MX // 2, NX // 2)
        x = 2.0 * float_iota(shape, 1) + parity
        put_rotation(wxi_ref, (parity,), 0, *cos_sin(x * float_iota(shape, 0)), False)
        shape = (NZ // 2, NZ)
        z = 4.0 * float_iota(shape, 0) + 2.0 * parity
        put_rotation(wzi_ref, (parity,), 0, *cos_sin(z * float_iota(shape, 1)), True)
    for chunk in range(NZ // Z_CHUNK):
        shape = (2 * Z_CHUNK, NZ)
        row = iota(shape, 0)
        kz = chunk * Z_CHUNK + jnp.where(row < Z_CHUNK, row, row + NZ - Z_CHUNK)
        angle = 2.0 * kz.astype(F32) * device_of(iota(shape, 1)).astype(F32)
        put_rotation(wz_ref, (), chunk * 4 * Z_CHUNK, *cos_sin(angle), False)
    for slot in range(2):
        shape = (NY, ND)
        q = device_of(iota(shape, 1))
        ky = 4 * q + slot + jnp.where(q < ND // 2, 1, 0)
        c, s = cos_sin(ky.astype(F32) * float_iota(shape, 0))
        weight = jnp.where(ky == MY // 2, NORM, 2.0 * NORM)
        s = jnp.where(ky == MY // 2, -1.0, s)
        put_parts(yb_ref, (), slice(0, NY), slice(256 * slot, 256 * slot + 128), c * weight)
        put_parts(yb_ref, (), slice(0, NY), slice(256 * slot + 128, 256 * slot + 256), -s * weight)
    for part, value in enumerate(slope_parts(NY)):
        slope_ref[part] = value
    for part, value in enumerate(slope_parts(NZ, device_of)):
        slope_z_ref[part, :, 0:NZ] = value
        slope_z_ref[part, :, NZ : 2 * NZ] = value


def outward_kernel(dens_hbm, table_hbm, filt_hbm, out_ref, plane_ref, dens_ref, table_ref, sems):
    dens_copy = pltpu.make_async_copy(dens_hbm, dens_ref, sems.at[0])
    table_copy = pltpu.make_async_copy(table_hbm, table_ref, sems.at[1])
    plane_copy = pltpu.make_async_copy(filt_hbm.at[:, 0, :], plane_ref, sems.at[2])
    dens_copy.start()
    table_copy.start()
    plane_copy.start()
    slope = slope_parts(NY)
    parity = parity_matrix(False)
    dens_copy.wait()
    for spin in range(2):
        field = dens_ref[spin * NY : (spin + 1) * NY, :]
        grad = dot3(*slope, *split(field))
        for part in range(2):
            rows = slice(part * 128, part * 128 + 128)
            put_rows(out_ref, spin * 4 + part * 2, OUT_ROWS, field[rows])
            put_rows(out_ref, 8 + spin * 4 + part * 2, OUT_ROWS, grad[rows])
    hi, lo = split(dens_ref[0:NY, :] + dens_ref[NY : 2 * NY, :])
    hi, lo = dot1(hi, parity), dot1(lo, parity)
    hi, lo = hi.astype(BF16), lo.astype(BF16)
    table_copy.wait()
    for s in range(4):
        rows = slice(s * ND, (s + 1) * ND)
        value = dot3(table_ref[0, rows, :], table_ref[1, rows, :], hi, lo)
        put_rows(out_ref, HART + s * 2, OUT_ROWS, value)
    plane_copy.wait()


LN2 = math.log(2.0)


def pw_piece(powers, params):
    root, radius, cube, square = powers
    scale = 2.0 * params[0]
    t1, t2 = (scale * params[2]) * root, (scale * params[3]) * radius
    t3, t4 = (scale * params[4]) * cube, (scale * params[5]) * square
    series = (t1 + t2) + (t3 + t4)
    slope = (series + t4) + 0.5 * (t3 - t1)
    more = series + 1.0
    inv = 1.0 / (series * more)
    logarithm = jnp.log(1.0 + inv * more)
    tilt = (-scale * params[1]) * radius
    front = tilt - scale
    return front * logarithm, tilt * logarithm - (front * slope) * inv


def exchange_piece(twice, inv_root, sigma):
    inv2 = inv_root * inv_root
    inv4 = inv2 * inv2
    root = twice * inv2
    front = -0.75 * (3.0 / math.pi) ** (1.0 / 3.0)
    unit = 1.0 / (3.0 * math.pi**2) ** (2.0 / 3.0)
    damp = 1.0 / (1.0 + (MU_X / KAPPA * unit) * sigma * (inv4 * inv4))
    gain = KAPPA - KAPPA * damp
    scaled = front * root
    energy = twice * scaled * (1.0 + gain)
    d_dens = scaled * (4.0 / 3.0 + gain * (4.0 / 3.0 - (8.0 / 3.0) * damp))
    d_sigma = (front * MU_X * unit) * (damp * damp) * inv4
    return energy, d_dens, d_sigma, root


def xc_point(up, down, sigma_uu, sigma_ud, sigma_dd):
    twice_up, twice_down = up + up, down + down
    inv_up = jnp.exp2(jnp.log(twice_up) * (-1.0 / (3.0 * LN2)))
    inv_down = jnp.exp2(jnp.log(twice_down) * (-1.0 / (3.0 * LN2)))
    e_up, d_up, d_uu, root_up = exchange_piece(twice_up, inv_up, sigma_uu)
    e_down, d_down, d_dd, root_down = exchange_piece(twice_down, inv_down, sigma_dd)
    dens = up + down
    sixth = jnp.exp2(jnp.log(dens) * (-1.0 / (6.0 * LN2)))
    inv_third = sixth * sixth
    inv_two = inv_third * inv_third
    third = dens * inv_two
    inv_dens = inv_two * inv_third
    plus = twice_up * inv_dens
    minus = twice_down * inv_dens
    zeta = 0.5 * (plus - minus)
    plus_cube = root_up * inv_third
    minus_cube = root_down * inv_third
    f_scale = 1.0 / (2.0 ** (4.0 / 3.0) - 2.0)
    f = (plus * plus_cube + minus * minus_cube) * f_scale - 2.0 * f_scale
    f_slope = (plus_cube - minus_cube) * (4.0 / 3.0 * f_scale)
    root = (3.0 / (4.0 * math.pi)) ** (1.0 / 6.0) * sixth
    radius = root * root
    powers = (root, radius, radius * root, radius * radius)
    e0, e0_d = pw_piece(powers, PARAMS_UNPOL)
    e1, e1_d = pw_piece(powers, PARAMS_POL)
    ac, ac_d = pw_piece(powers, PARAMS_STIFF)
    z2 = zeta * zeta
    z4 = z2 * z2
    one_z4 = z4 * (1.0 / FZ_CURV) - 1.0 / FZ_CURV
    f_z4 = f * z4
    f_one = f * one_z4
    diff = e1 - e0
    local = e0 + ac * f_one + diff * f_z4
    local_r = e0_d + ac_d * f_one + (e1_d - e0_d) * f_z4
    local_z = (ac * one_z4 + diff * z4) * f_slope + (ac * (1.0 / FZ_CURV) + diff) * (
        4.0 * f * z2 * zeta
    )
    phi2 = plus_cube * plus_cube + minus_cube * minus_cube
    inv_phi2 = 1.0 / phi2
    inv_sq = inv_phi2 * inv_phi2
    phi_log_slope = (third * (inv_up - inv_down)) * ((2.0 / 3.0) * inv_phi2)
    g3 = (GAMMA_C / 8.0) * (phi2 * phi2) * phi2
    grow = jnp.exp2(local * (inv_sq * inv_phi2) * (-8.0 / (GAMMA_C * LN2)))
    weight_a = (BETA_C / GAMMA_C) / (grow - 1.0)
    sigma = (sigma_uu + sigma_dd) + (sigma_ud + sigma_ud)
    ct = 4.0 * math.pi / (16.0 * (3.0 * math.pi**2) ** (1.0 / 3.0))
    kt = (ct * inv_third) * (inv_dens * inv_dens) * inv_sq
    t2 = sigma * kt
    w = weight_a * t2
    num = 1.0 + w
    den = num + w * w
    add = (BETA_C / GAMMA_C) * t2 * num
    both = den + add
    inv_both = 1.0 / (den * both)
    h = g3 * jnp.log(1.0 + add * (inv_both * both))
    h_t = ((BETA_C / GAMMA_C) * g3) * ((num + w) * inv_both)
    h_a = -((w * w) * w) * ((1.0 + num) * grow) * inv_both
    total = local + h
    ht_t2 = h_t * t2
    one_ha = 1.0 + h_a
    d_n = total - one_ha * ((1.0 / 3.0) * local_r) - (7.0 / 3.0) * ht_t2
    d_z = one_ha * local_z + phi_log_slope * (3.0 * (h - h_a * local) - (ht_t2 + ht_t2))
    d_sigma = 2.0 * (dens * h_t * kt)
    energy = 0.5 * (e_up + e_down) + dens * total
    return (
        energy,
        d_up + d_n + minus * d_z,
        d_down + d_n - plus * d_z,
        d_uu + d_sigma,
        d_sigma,
        d_dd + d_sigma,
    )


def slope_along_z(slope_z_ref, hi, lo):
    both = jnp.concatenate([hi, lo], axis=0)
    return dot1(slope_z_ref[0], both) + dot1(slope_z_ref[1], both)


def slope_along_x(slope_ref, hi, lo):
    return -dot3(hi, lo, slope_ref[0], slope_ref[1])


def xc_steps(in_ref, slope_ref, slope_z_ref, out_ref, total_ref, dens, gz, gy, gx):
    def gradients(part):
        rows = slice(part * 128, part * 128 + 128)
        for spin in range(2):
            field = get_rows(in_ref, spin * 4 + part * 2, OUT_ROWS)
            dens[spin, rows, :] = field
            gy[spin, rows, :] = get_rows(in_ref, 8 + spin * 4 + part * 2, OUT_ROWS)
            hi, lo = split(field)
            gz[spin, rows, :] = slope_along_z(slope_z_ref, hi, lo)
            gx[spin, rows, :] = slope_along_x(slope_ref, hi, lo)

    def points(i):
        rows = slice(i * XC_ROWS, (i + 1) * XC_ROWS)
        zu, zd = gz[0, rows, :], gz[1, rows, :]
        yu, yd = gy[0, rows, :], gy[1, rows, :]
        xu, xd = gx[0, rows, :], gx[1, rows, :]
        energy, d_up, d_down, d_uu, d_ud, d_dd = xc_point(
            dens[0, rows, :],
            dens[1, rows, :],
            zu * zu + yu * yu + xu * xu,
            zu * zd + yu * yd + xu * xd,
            zd * zd + yd * yd + xd * xd,
        )
        dens[0, rows, :] = d_up
        dens[1, rows, :] = d_down
        for ref, gu, gd in ((gz, zu, zd), (gy, yu, yd), (gx, xu, xd)):
            ref[0, rows, :] = d_uu * gu + d_ud * gd
            ref[1, rows, :] = d_dd * gd + d_ud * gu
        folded = sum(energy[r : r + 8] for r in range(0, XC_ROWS, 8))
        total_ref[...] = folded if i == 0 else total_ref[...] + folded

    def divergence(part):
        rows = slice(part * 128, part * 128 + 128)
        for spin in range(2):
            div = slope_along_z(slope_z_ref, *split(gz[spin, rows, :]))
            div = div + slope_along_x(slope_ref, *split(gx[spin, rows, :]))
            put_rows(out_ref, spin * 4 + part * 2, BACK_ROWS, dens[spin, rows, :] - div)
            put_rows(out_ref, 8 + spin * 4 + part * 2, BACK_ROWS, gy[spin, rows, :])

    steps = []
    for part in range(2):
        steps.append(lambda part=part: gradients(part))
        for i in range(part * 128 // XC_ROWS, (part + 1) * 128 // XC_ROWS):
            steps.append(lambda i=i: points(i))
        steps.append(lambda part=part: divergence(part))
    return steps


def hartree_steps(
    in_ref, filt_ref, other_ref, weight_ref, wx_ref, wz_ref, wzi_ref, wxi_ref, out_ref, power_ref,
    xp, sums, back,
):
    def forward_x(slot, conjugate):
        parts = []
        for parity in range(2):
            base = HART + 4 * slot + parity
            real = in_ref[pl.ds(base, ND, stride=OUT_ROWS), :]
            imag = in_ref[pl.ds(base + 2, ND, stride=OUT_ROWS), :]
            both = jnp.concatenate([real, -imag if conjugate else imag], axis=1)
            parts.append(dot3(*split(both), wx_ref[parity, 0], wx_ref[parity, 1]))
        place = 2 if conjugate else slot
        for half, value in ((0, parts[0] + parts[1]), (1, parts[0] - parts[1])):
            cols = slice(half * 256, half * 256 + 256)
            hi, lo = split(value)
            xp[place, 0, 0:128, cols] = hi[:, 0:256]
            xp[place, 0, 128:256, cols] = hi[:, 256:512]
            xp[place, 1, 0:128, cols] = lo[:, 0:256]
            xp[place, 1, 128:256, cols] = lo[:, 256:512]

    def filtered(slot, c):
        rows = slice(c * 128, c * 128 + 128)
        spec = dot3(wz_ref[0, rows, :], wz_ref[1, rows, :], xp[slot, 0], xp[slot, 1])
        if slot == 0:
            mirror = dot3(wz_ref[0, rows, :], wz_ref[1, rows, :], xp[2, 0], xp[2, 1])
        planes = []
        for high in range(2):
            place = slice(high * NZ + c * Z_CHUNK, high * NZ + (c + 1) * Z_CHUNK)
            own = filt_ref[slot, place, :]
            if slot == 0:
                swap = (own - other_ref[place, :]) * weight_ref[2]
                planes.append((own - swap, swap))
            else:
                planes.append((own, None))
        acc = None
        first = slot == 0 and c == 0
        for kind in range(2):
            pair = []
            for high in range(2):
                at = slice(kind * 64 + high * 32, kind * 64 + high * 32 + 32)
                value = spec[at] * planes[high][0]
                if slot == 0:
                    value = value + mirror[at] * planes[high][1]
                power = spec[at] * value
                power = power[0:8] + power[8:16] + (power[16:24] + power[24:32])
                acc = power if acc is None else acc + power
                pair.append(value)
            dest = slice(kind * NZ + c * Z_CHUNK, kind * NZ + (c + 1) * Z_CHUNK)
            for parity, value in ((0, pair[0] + pair[1]), (1, pair[0] - pair[1])):
                hi, lo = split(value)
                sums[slot, parity, 0, dest, :] = hi
                sums[slot, parity, 1, dest, :] = lo
        acc = weight_ref[slot] * acc
        power_ref[...] = acc if first else power_ref[...] + acc

    def back_z(slot, parity):
        src = sums.at[slot, parity]
        grid = dot3(wzi_ref[parity, 0], wzi_ref[parity, 1], src[0], src[1])
        for sign in range(2):
            a, b = grid[:, 0:256], grid[:, 256:512]
            hi, lo = split(a + b if sign == 0 else a - b)
            for part, value in ((0, hi), (1, lo)):
                rows = slice(parity * 64, parity * 64 + 64)
                back[slot, sign, part, rows, 0:256] = value[0:64]
                back[slot, sign, part, rows, 256:512] = value[64:128]

    def back_x(slot, sign):
        src = back.at[slot, sign]
        value = dot3(src[0], src[1], wxi_ref[sign, 0], wxi_ref[sign, 1])
        for parity in range(2):
            for kind in range(2):
                put_rows(
                    out_ref,
                    parity * 64 * BACK_ROWS + HART + slot * 4 + kind * 2 + sign,
                    BACK_ROWS,
                    value[parity * 64 : parity * 64 + 64, kind * 128 : kind * 128 + 128],
                    count=64,
                )

    kinds = {
        "x": lambda slot, i: forward_x(slot, i == 1),
        "z": filtered,
        "b": back_z,
        "o": back_x,
    }
    return [
        (name, lambda name=name: kinds[name[0]](int(name[1]), int(name[2])))
        for name in HART_ORDER
    ]


def middle_kernel(
    first_ref, weight_ref, in_ref, other_ref, slope_ref, slope_z_ref, filt_hbm, wx_hbm, wz_hbm, wzi_hbm,
    wxi_hbm, out_ref, filt_ref, wx_ref, wz_ref, wzi_ref, wxi_ref, dens, gz, gy, gx, xp, sums, back,
    total_ref, power_ref, sems,
):
    moves = [(wx_hbm, wx_ref), (wz_hbm, wz_ref)]
    moves += [
        (filt_hbm.at[:, first_ref[0] + slot, :], filt_ref.at[slot]) for slot in range(2)
    ]
    moves += [(wzi_hbm, wzi_ref), (wxi_hbm, wxi_ref)]
    copies = [
        pltpu.make_async_copy(source, target, sems.at[i]) for i, (source, target) in enumerate(moves)
    ]
    for copy in copies:
        copy.start()
    xc = xc_steps(in_ref, slope_ref, slope_z_ref, out_ref, total_ref, dens, gz, gy, gx)
    hartree = hartree_steps(
        in_ref, filt_ref, other_ref, weight_ref, wx_ref, wz_ref, wzi_ref, wxi_ref, out_ref,
        power_ref, xp, sums, back,
    )
    for step in xc[:XC_AHEAD]:
        step()
    xc = xc[XC_AHEAD:]
    done = 0
    waits = {"x00": (0,), "z00": (1, 2), "z10": (3,), "b00": (4,), "o00": (5,)}
    for i, (name, step) in enumerate(hartree):
        for copy in waits.get(name, ()):
            copies[copy].wait()
        step()
        upto = min(len(xc), -(-(i + 1) * len(xc) // XC_SPREAD))
        for other in xc[done:upto]:
            other()
        done = max(done, upto)
    for other in xc[done:]:
        other()
    energies = jnp.where(
        iota((ND, 128), 1) < 64, jnp.sum(total_ref[...]), jnp.sum(power_ref[...])
    )
    put_rows(out_ref, BACK_ROWS - 1, BACK_ROWS, energies)


def homeward_kernel(in_ref, yb_ref, slope_ref, out_ref, energy_ref):
    field = jnp.concatenate(
        [get_rows(in_ref, HART + 2 * s, BACK_ROWS) for s in range(4)], axis=0
    )
    grid = dot3(yb_ref[0], yb_ref[1], *split(field))
    hi, lo = split(grid)
    parity = parity_matrix(True)
    hartree = dot1(hi, parity) + dot1(lo, parity)
    for spin in range(2):
        flux, rest = (
            jnp.concatenate(
                [get_rows(in_ref, base + spin * 4 + part * 2, BACK_ROWS) for part in range(2)],
                axis=0,
            )
            for base in (8, 0)
        )
        rows = slice(spin * NY, (spin + 1) * NY)
        out_ref[rows, :] = rest + hartree - dot3(slope_ref[0], slope_ref[1], *split(flux))
    row = jnp.sum(in_ref[pl.ds(BACK_ROWS - 1, ND, stride=BACK_ROWS), :], axis=0, keepdims=True)
    first = iota((1, 128), 1) < 64
    energy_ref[0] = jnp.sum(jnp.where(first, row, 0.0)) * (1.0 / (64.0 * CELLS))
    energy_ref[1] = jnp.sum(jnp.where(first, 0.0, row)) * (0.5 * NORM / (64.0 * CELLS))


def call(kernel, outs, in_specs, flops, scratch=(), smem_out=(), limit=40):
    specs = [SMEM if i in smem_out else VMEM for i in range(len(outs))]
    return pl.pallas_call(
        kernel,
        out_shape=list(outs),
        in_specs=in_specs,
        out_specs=specs,
        scratch_shapes=list(scratch),
        cost_estimate=pl.CostEstimate(flops=flops, bytes_accessed=4 << 20, transcendentals=0),
        compiler_params=pltpu.CompilerParams(vmem_limit_bytes=limit << 20),
    )


def in_hbm(value):
    return pltpu.with_memory_space_constraint(value, pltpu.HBM)


def arr(*shape, dtype=F32):
    return jax.ShapeDtypeStruct(shape, dtype)


def exchange(value, rows, group):
    shaped = value.reshape(ND * rows // group, group, 128)
    out = lax.all_to_all(shaped, BLOCKS, split_axis=0, concat_axis=0, tiled=True)
    return out.reshape(ND * rows, 128)


def per_device(density, kernel_hat):
    q = lax.axis_index(GZ)
    kernel_hat = in_hbm(kernel_hat)
    outward, plane = call(
        outward_kernel,
        [arr(ND * OUT_ROWS, 128), arr(MZ, MX)],
        [HBM, HBM, HBM],
        400_000_000,
        scratch=[
            pltpu.VMEM((2 * NY, NX), F32),
            pltpu.VMEM((2, 4 * ND, NY), BF16),
            pltpu.SemaphoreType.DMA((3,)),
        ],
    )(in_hbm(density.reshape(2 * NY, NX)), in_hbm(jnp.asarray(y_forward())), kernel_hat)
    other = lax.ppermute(plane, GZ, [(0, PAIR)])
    arrived = exchange(outward, OUT_ROWS, 8)
    shapes = [(2, 2, NX, MX), (2, 2 * MZ, 2 * NZ), (2, 2, NZ, 2 * NZ), (2, 2, MX, NX)]
    wx, wz, wzi, wxi, yb, slope, slope_z = call(
        tables_kernel,
        [arr(*shape, dtype=BF16) for shape in shapes]
        + [
            arr(2, NY, 4 * ND, dtype=BF16),
            arr(2, NY, NY, dtype=BF16),
            arr(2, NZ, 2 * NZ, dtype=BF16),
        ],
        [],
        2_000_000_000,
    )()
    start = jnp.where(q < ND // 2, 1, 0).astype(jnp.int32).reshape(1)
    weights = jnp.stack(
        [jnp.where(q == PAIR, 1.0, 2.0), jnp.full((), 2.0), jnp.where(q == PAIR, 0.5, 0.0)]
    ).astype(F32)
    field = pltpu.VMEM((2, 256, NX), F32)
    (back,) = call(
        middle_kernel,
        [arr(ND * BACK_ROWS, 128)],
        [SMEM, SMEM] + [VMEM] * 4 + [HBM] * 5,
        8_000_000_000,
        scratch=[pltpu.VMEM((2, MZ, MX), F32)]
        + [pltpu.VMEM(shape, BF16) for shape in shapes]
        + [field] * 4
        + [
            pltpu.VMEM((3, 2, 256, 512), BF16),
            pltpu.VMEM((2, 2, 2, 256, 512), BF16),
            pltpu.VMEM((2, 2, 2, 128, 512), BF16),
            pltpu.VMEM((8, NX), F32),
            pltpu.VMEM((8, MX), F32),
            pltpu.SemaphoreType.DMA((6,)),
        ],
    )(start, weights, arrived, other, slope, slope_z, kernel_hat, *map(in_hbm, (wx, wz, wzi, wxi)))
    returned = exchange(back, BACK_ROWS, 1)
    potential, energies = call(
        homeward_kernel,
        [arr(2 * NY, NX), arr(2)],
        [VMEM] * 3,
        1_000_000_000,
        smem_out=(1,),
    )(returned, yb, slope)
    return potential.reshape(2, 1, NY, NX), energies


def solution(mesh):
    torus = Mesh(mesh.devices.reshape(4, 4, 4, 2), GZ)
    placed = (P(None, GZ, None, None), P(None, GZ, None))
    return jax.shard_map(
        per_device,
        mesh=torus,
        in_specs=placed,
        out_specs=(P(None, GZ, None, None), P()),
        check_vma=False,
    )
```

profile of v0, /device:TPU:1, one launch (start us, length us, event | category | flops | bytes accessed | tf_op | source)
XLA Modules:
  0.0 78.7 jit_solution(111839319862280428)
XLA Ops:
  0.6 3.1 %shard_map.50 = (f32[3072,128]{1,0:T(8,128)}, f32[256,512]{1,0:T(8,128)S(1)}) custom-call(f32[512,256]{1,0:T(8,128)} %bitcast.16, bf16[2,512,256]{2,1,0:T(8,128)(2,1)} %constant.39.clone.table_hbm, f32[256,4,512]{2,1,0:T(4,128)} %filt_hbm.3), custom_call_target="tpu_custom_call" | custom-call | flops 400000000 | bytes 4194304 | tf_op jit(solution)/shard_map/pallas_call | solution.py:570
  3.8 11.5 %all-to-all-start = ((f32[384,8,128]{2,1,0:T(8,128)}), f32[384,8,128]{2,1,0:T(8,128)S(1)}, u32[]{:S(2)}, u32[]{:S(2)}) async-start(f32[384,8,128]{2,1,0:T(8,128)} %bitcast.4), calls=%async_computation | async-start | bytes 3145728 | tf_op jit(solution)/shard_map/all_to_all | solution.py:563
  15.3 0.7 collective-permute-start
  16.0 0.1 pad_maximum_fusion.weight_ref
  16.1 2.1 %shard_map.51 = (bf16[2,2,256,512]{3,2,1,0:T(8,128)(2,1)S(1)}, bf16[2,512,256]{2,1,0:T(8,128)(2,1)S(1)}, bf16[2,2,128,256]{3,2,1,0:T(8,128)(2,1)S(1)}, bf16[2,2,...) custom-call(), custom_call_target="tpu_custom_call" | custom-call | flops 2000000000 | bytes 4194304 | tf_op jit(solution)/shard_map/pallas_call | solution.py:584
  18.2 0.0 copy-start
  18.2 1.0 %copy-done = bf16[2,2,256,512]{3,2,1,0:T(8,128)(2,1)} copy-done((bf16[2,2,256,512]{3,2,1,0:T(8,128)(2,1)}, bf16[2,2,256,512]{3,2,1,0:T(8,128)(2,1)S(1)}, u32[]{:S(2)}) %copy-start) | copy-done | bytes 1048600
  19.1 0.0 copy-start.1
  19.1 1.0 %copy-done.1 = bf16[2,2,512,256]{3,2,1,0:T(8,128)(2,1)} copy-done((bf16[2,2,512,256]{3,2,1,0:T(8,128)(2,1)}, bf16[2,2,512,256]{3,2,1,0:T(8,128)(2,1)S(1)}, u32[]{:S(2)}) %copy-start.1) | copy-done | bytes 1048600
  20.1 0.0 copy-start.2
  20.1 0.8 %copy-done.2 = bf16[2,512,256]{2,1,0:T(8,128)(2,1)} copy-done((bf16[2,512,256]{2,1,0:T(8,128)(2,1)}, bf16[2,512,256]{2,1,0:T(8,128)(2,1)S(1)}, u32[]{:S(2)}) %copy-start.2) | copy-done | bytes 524312
  20.9 0.0 copy-start.3
  20.9 0.7 copy-done.3
  21.6 0.0 collective-permute-done.other_ref
  21.6 16.5 %all-to-all-done = f32[384,8,128]{2,1,0:T(8,128)S(1)} async-done(((f32[384,8,128]{2,1,0:T(8,128)}), f32[384,8,128]{2,1,0:T(8,128)S(1)}, u32[]{:S(2)}, u32[]{:S(2)}) %all-to-all-start) | async-done | bytes 1572896 | tf_op jit(solution)/shard_map/all_to_all | solution.py:563
  38.1 7.6 %shard_map.52 = f32[3200,128]{1,0:T(8,128)S(1)} custom-call(s32[1]{0:T(128)} %bitcast.first_ref, f32[3]{0:T(128)S(1)} %pad_maximum_fusion.weight_ref, f32[3072,128]{1,0:T(8,128)S(1)} %bitcast.15, f32[256,512]{1,0:T(8,128)S(1)} %collective-permute-done.other_ref, bf16[2,256,256]{2,1,0:T(8,128)(2,1)S(1)} %get-tuple-element.15.slope_ref, ...), custom_call_target="tpu_custom_call" | custom-call | flops 8000000000 | bytes 4194304 | tf_op jit(solution)/shard_map/pallas_call | solution.py:600
  45.7 31.1 %all_to_all.10 = f32[3200,1,128]{2,1,0:T(1,128)S(1)} all-to-all(f32[3200,1,128]{2,1,0:T(1,128)S(1)} %bitcast.13), channel_id=1, replica_groups=mesh['gz_0'=4,'gz_1'=4,'gz_2'=4,'gz_3'=2] {'gz_3','gz_0','gz_1','gz_2'}, dimensions={0} | all-to-all | bytes 3276800 | tf_op jit(solution)/shard_map/all_to_all | solution.py:563
  76.8 1.9 %shard_map.53 = (f32[512,256]{1,0:T(8,128)}, f32[2]{0:T(128)}) custom-call(f32[3200,128]{1,0:T(8,128)S(1)} %bitcast.14, bf16[2,256,512]{2,1,0:T(8,128)(2,1)S(1)} %get-tuple-element.21.yb_ref, bf16[2,256,256]{2,1,0:T(8,128)(2,1)S(1)} %get-tuple-element.15.slope_ref), custom_call_target="tpu_custom_call" | custom-call | flops 1000000000 | bytes 4194304 | tf_op jit(solution)/shard_map/pallas_call | solution.py:618
Async XLA Ops:
  3.8 34.3 %all-to-all-start = ((f32[384,8,128]{2,1,0:T(8,128)}), f32[384,8,128]{2,1,0:T(8,128)S(1)}, u32[]{:S(2)}, u32[]{:S(2)}) async-start(f32[384,8,128]{2,1,0:T(8,128)} %bitcast.4), calls=%async_computation | async-start | bytes 3145728 | tf_op jit(solution)/shard_map/all_to_all | solution.py:563
  15.3 6.3 %collective-permute-start = (f32[256,512]{1,0:T(8,128)S(1)}, f32[256,512]{1,0:T(8,128)S(1)}, u32[]{:S(2)}, u32[]{:S(2)}) collective-permute-start(f32[256,512]{1,0:T(8,128)S(1)} %get-tuple-element.14), channel_id=1, source_target_pairs={{0,64}} | collective-permute-start | bytes 1572872 | tf_op jit(solution)/shard_map/ppermute | solution.py:581
  18.2 1.0 %copy-start = (bf16[2,2,256,512]{3,2,1,0:T(8,128)(2,1)}, bf16[2,2,256,512]{3,2,1,0:T(8,128)(2,1)S(1)}, u32[]{:S(2)}) copy-start(bf16[2,2,256,512]{3,2,1,0:T(8,128)(2,1)S(1)} %get-tuple-element.17.wx_hbm) | copy-start | bytes 3145732
  19.1 1.0 %copy-start.1 = (bf16[2,2,512,256]{3,2,1,0:T(8,128)(2,1)}, bf16[2,2,512,256]{3,2,1,0:T(8,128)(2,1)S(1)}, u32[]{:S(2)}) copy-start(bf16[2,2,512,256]{3,2,1,0:T(8,128)(2,1)S(1)} %get-tuple-element.20.wxi_hbm) | copy-start | bytes 3145732
  20.1 0.8 %copy-start.2 = (bf16[2,512,256]{2,1,0:T(8,128)(2,1)}, bf16[2,512,256]{2,1,0:T(8,128)(2,1)S(1)}, u32[]{:S(2)}) copy-start(bf16[2,512,256]{2,1,0:T(8,128)(2,1)S(1)} %get-tuple-element.18.wz_hbm) | copy-start | bytes 1572868
  20.9 0.7 copy-start.3
where the time goes:
time: 79 us; the launch traced here: 78.7 us
  blocking collectives  31.1 us (39%)
  waiting for transfers between devices  16.5 us (21%)
  Pallas kernels  14.7 us (19%)
  starting transfers between devices  12.2 us (15%)
  local copies, waits for them, and re-layouts  3.44 us (4%)
    all_to_all x1, blocking collectives, exchange(): lax.all_to_all(shaped, BLOCKS, split_axis=0, concat_axis=0, tiled=True)  31.1 us
    all_to_all x1, waiting for transfers between devices, exchange(): lax.all_to_all(shaped, BLOCKS, split_axis=0, concat_axis=0, tiled=True)  16.5 us
    all_to_all x1, starting transfers between devices, exchange(): lax.all_to_all(shaped, BLOCKS, split_axis=0, concat_axis=0, tiled=True)  11.5 us
    pallas_call x1, Pallas kernels, per_device(): call(middle_kernel, [arr(ND * BACK_ROWS, 128)], [SMEM, SMEM] + [VMEM] * 4...  7.58 us
    unnamed x8, local copies, waits for them, and re-layouts  3.44 us
    pallas_call x1, Pallas kernels, per_device(): call(outward_kernel, [arr(ND * OUT_ROWS, 128), arr(MZ, MX)], [HBM, HBM, H...  3.15 us
    pallas_call x1, Pallas kernels, per_device(): call(tables_kernel, [arr(*shape, dtype=BF16) for shape in shapes] + [arr(...  2.09 us
    pallas_call x1, Pallas kernels, per_device(): call(homeward_kernel, [arr(2 * NY, NX), arr(2)], [VMEM] * 3, 1000000000,...  1.92 us
  transfers between devices with their start and end apart: 2, of which 1 were waited for; matrix products, arithmetic and copies ran while one was open for 0% of the time, Pallas kernels for 3%

commit v1 on v0

--- a/solution.py
+++ b/solution.py
@@ -33,14 +33,12 @@
 BACK_ROWS = 25
 PAIR = ND // 2
 CELLS = NZ * NY * NX
-Z_CHUNK = 32
+Z_CHUNK = 64
 XC_ROWS = 8
 XC_AHEAD = 12
-XC_SPREAD = 19
+XC_SPREAD = 16
 HART_ORDER = (
-    "x00", "x01", "x10", "z00", "z01", "z02", "z03", "z10",
-    "b00", "z11", "b01", "z12", "o00", "z13", "o01", "b10",
-    "b11", "o10", "o11",
+    "x00", "x01", "z00", "z01", "z10", "b00", "b01", "z11", "o00", "o01", "b10", "b11", "o10", "o11",
 )
 NORM = 1.0 / (MX * MY * MZ)
 VMEM = pl.BlockSpec(memory_space=pltpu.VMEM)
@@ -382,27 +380,33 @@
 
 def hartree_steps(
     in_ref, filt_ref, other_ref, weight_ref, wx_ref, wz_ref, wzi_ref, wxi_ref, out_ref, power_ref,
-    xp, sums, back,
+    half_ref, xp, sums, back,
 ):
-    def forward_x(slot, conjugate):
-        parts = []
-        for parity in range(2):
+    def forward_x(_slot, parity):
+        stack = []
+        for slot, sign in ((0, 1), (1, 1), (0, -1)):
             base = HART + 4 * slot + parity
             real = in_ref[pl.ds(base, ND, stride=OUT_ROWS), :]
             imag = in_ref[pl.ds(base + 2, ND, stride=OUT_ROWS), :]
-            both = jnp.concatenate([real, -imag if conjugate else imag], axis=1)
-            parts.append(dot3(*split(both), wx_ref[parity, 0], wx_ref[parity, 1]))
-        place = 2 if conjugate else slot
-        for half, value in ((0, parts[0] + parts[1]), (1, parts[0] - parts[1])):
+            stack.append(jnp.concatenate([real, imag if sign > 0 else -imag], axis=1))
+        both = jnp.concatenate(stack, axis=0)
+        value = dot3(*split(both), wx_ref[parity, 0], wx_ref[parity, 1])
+        if parity == 0:
+            half_ref[...] = value
+            return
+        for half in range(2):
             cols = slice(half * 256, half * 256 + 256)
-            hi, lo = split(value)
-            xp[place, 0, 0:128, cols] = hi[:, 0:256]
-            xp[place, 0, 128:256, cols] = hi[:, 256:512]
-            xp[place, 1, 0:128, cols] = lo[:, 0:256]
-            xp[place, 1, 128:256, cols] = lo[:, 256:512]
+            whole = half_ref[...] + value if half == 0 else half_ref[...] - value
+            hi, lo = split(whole)
+            for place in range(3):
+                rows = slice(place * 128, place * 128 + 128)
+                xp[place, 0, 0:128, cols] = hi[rows, 0:256]
+                xp[place, 0, 128:256, cols] = hi[rows, 256:512]
+                xp[place, 1, 0:128, cols] = lo[rows, 0:256]
+                xp[place, 1, 128:256, cols] = lo[rows, 256:512]
 
     def filtered(slot, c):
-        rows = slice(c * 128, c * 128 + 128)
+        rows = slice(c * 4 * Z_CHUNK, (c + 1) * 4 * Z_CHUNK)
         spec = dot3(wz_ref[0, rows, :], wz_ref[1, rows, :], xp[slot, 0], xp[slot, 1])
         if slot == 0:
             mirror = dot3(wz_ref[0, rows, :], wz_ref[1, rows, :], xp[2, 0], xp[2, 1])
@@ -420,12 +424,13 @@
         for kind in range(2):
             pair = []
             for high in range(2):
-                at = slice(kind * 64 + high * 32, kind * 64 + high * 32 + 32)
+                start = (2 * kind + high) * Z_CHUNK
+                at = slice(start, start + Z_CHUNK)
                 value = spec[at] * planes[high][0]
                 if slot == 0:
                     value = value + mirror[at] * planes[high][1]
                 power = spec[at] * value
-                power = power[0:8] + power[8:16] + (power[16:24] + power[24:32])
+                power = sum(power[r : r + 8] for r in range(0, Z_CHUNK, 8))
                 acc = power if acc is None else acc + power
                 pair.append(value)
             dest = slice(kind * NZ + c * Z_CHUNK, kind * NZ + (c + 1) * Z_CHUNK)
@@ -461,7 +466,7 @@
                 )
 
     kinds = {
-        "x": lambda slot, i: forward_x(slot, i == 1),
+        "x": forward_x,
         "z": filtered,
         "b": back_z,
         "o": back_x,
@@ -475,7 +480,7 @@
 def middle_kernel(
     first_ref, weight_ref, in_ref, other_ref, slope_ref, slope_z_ref, filt_hbm, wx_hbm, wz_hbm, wzi_hbm,
     wxi_hbm, out_ref, filt_ref, wx_ref, wz_ref, wzi_ref, wxi_ref, dens, gz, gy, gx, xp, sums, back,
-    total_ref, power_ref, sems,
+    total_ref, power_ref, half_ref, sems,
 ):
     moves = [(wx_hbm, wx_ref), (wz_hbm, wz_ref)]
     moves += [
@@ -490,7 +495,7 @@
     xc = xc_steps(in_ref, slope_ref, slope_z_ref, out_ref, total_ref, dens, gz, gy, gx)
     hartree = hartree_steps(
         in_ref, filt_ref, other_ref, weight_ref, wx_ref, wz_ref, wzi_ref, wxi_ref, out_ref,
-        power_ref, xp, sums, back,
+        power_ref, half_ref, xp, sums, back,
     )
     for step in xc[:XC_AHEAD]:
         step()
@@ -611,6 +616,7 @@
             pltpu.VMEM((2, 2, 2, 128, 512), BF16),
             pltpu.VMEM((8, NX), F32),
             pltpu.VMEM((8, MX), F32),
+            pltpu.VMEM((3 * ND, MX), F32),
             pltpu.SemaphoreType.DMA((6,)),
         ],
     )(start, weights, arrived, other, slope, slope_z, kernel_hat, *map(in_hbm, (wx, wz, wzi, wxi)))

time: 79 us -> 78.9 us (level)
  no operation moved by 1% of the time
where the time goes in v1:
time: 78.9 us; the launch traced here: 78.7 us
  blocking collectives  31.1 us (39%)
  waiting for transfers between devices  16.5 us (21%)
  Pallas kernels  14.7 us (19%)
  starting transfers between devices  12.2 us (15%)
  local copies, waits for them, and re-layouts  3.44 us (4%)
    all_to_all x1, blocking collectives, exchange(): lax.all_to_all(shaped, BLOCKS, split_axis=0, concat_axis=0, tiled=True)  31.1 us
    all_to_all x1, waiting for transfers between devices, exchange(): lax.all_to_all(shaped, BLOCKS, split_axis=0, concat_axis=0, tiled=True)  16.5 us
    all_to_all x1, starting transfers between devices, exchange(): lax.all_to_all(shaped, BLOCKS, split_axis=0, concat_axis=0, tiled=True)  11.5 us
    pallas_call x1, Pallas kernels, per_device(): call(middle_kernel, [arr(ND * BACK_ROWS, 128)], [SMEM, SMEM] + [VMEM] * 4...  7.53 us
    unnamed x8, local copies, waits for them, and re-layouts  3.44 us
    pallas_call x1, Pallas kernels, per_device(): call(outward_kernel, [arr(ND * OUT_ROWS, 128), arr(MZ, MX)], [HBM, HBM, H...  3.15 us
    pallas_call x1, Pallas kernels, per_device(): call(tables_kernel, [arr(*shape, dtype=BF16) for shape in shapes] + [arr(...  2.1 us
    pallas_call x1, Pallas kernels, per_device(): call(homeward_kernel, [arr(2 * NY, NX), arr(2)], [VMEM] * 3, 1000000000,...  1.92 us
  transfers between devices with their start and end apart: 2, of which 1 were waited for; matrix products, arithmetic and copies ran while one was open for 0% of the time, Pallas kernels for 3%

profile of v1, /device:TPU:1, one launch (start us, length us, event | category | flops | bytes accessed | tf_op | source)
XLA Modules:
  0.0 78.7 jit_solution(10027521731742977969)
XLA Ops:
  0.6 3.1 %shard_map.50 = (f32[3072,128]{1,0:T(8,128)}, f32[256,512]{1,0:T(8,128)S(1)}) custom-call(f32[512,256]{1,0:T(8,128)} %bitcast.16, bf16[2,512,256]{2,1,0:T(8,128)(2,1)} %constant.39.clone.table_hbm, f32[256,4,512]{2,1,0:T(4,128)} %filt_hbm.3), custom_call_target="tpu_custom_call" | custom-call | flops 400000000 | bytes 4194304 | tf_op jit(solution)/shard_map/pallas_call | solution.py:575
  3.8 11.5 %all-to-all-start = ((f32[384,8,128]{2,1,0:T(8,128)}), f32[384,8,128]{2,1,0:T(8,128)S(1)}, u32[]{:S(2)}, u32[]{:S(2)}) async-start(f32[384,8,128]{2,1,0:T(8,128)} %bitcast.4), calls=%async_computation | async-start | bytes 3145728 | tf_op jit(solution)/shard_map/all_to_all | solution.py:568
  15.3 0.7 collective-permute-start
  16.0 0.1 pad_maximum_fusion.weight_ref
  16.1 2.1 %shard_map.51 = (bf16[2,2,256,512]{3,2,1,0:T(8,128)(2,1)S(1)}, bf16[2,512,256]{2,1,0:T(8,128)(2,1)S(1)}, bf16[2,2,128,256]{3,2,1,0:T(8,128)(2,1)S(1)}, bf16[2,2,...) custom-call(), custom_call_target="tpu_custom_call" | custom-call | flops 2000000000 | bytes 4194304 | tf_op jit(solution)/shard_map/pallas_call | solution.py:589
  18.2 0.0 copy-start
  18.2 1.0 %copy-done = bf16[2,2,256,512]{3,2,1,0:T(8,128)(2,1)} copy-done((bf16[2,2,256,512]{3,2,1,0:T(8,128)(2,1)}, bf16[2,2,256,512]{3,2,1,0:T(8,128)(2,1)S(1)}, u32[]{:S(2)}) %copy-start) | copy-done | bytes 1048600
  19.1 0.0 copy-start.1
  19.2 1.0 %copy-done.1 = bf16[2,2,512,256]{3,2,1,0:T(8,128)(2,1)} copy-done((bf16[2,2,512,256]{3,2,1,0:T(8,128)(2,1)}, bf16[2,2,512,256]{3,2,1,0:T(8,128)(2,1)S(1)}, u32[]{:S(2)}) %copy-start.1) | copy-done | bytes 1048600
  20.1 0.0 copy-start.2
  20.1 0.8 %copy-done.2 = bf16[2,512,256]{2,1,0:T(8,128)(2,1)} copy-done((bf16[2,512,256]{2,1,0:T(8,128)(2,1)}, bf16[2,512,256]{2,1,0:T(8,128)(2,1)S(1)}, u32[]{:S(2)}) %copy-start.2) | copy-done | bytes 524312
  20.9 0.0 copy-start.3
  20.9 0.7 copy-done.3
  21.6 0.0 collective-permute-done.other_ref
  21.6 16.5 %all-to-all-done = f32[384,8,128]{2,1,0:T(8,128)S(1)} async-done(((f32[384,8,128]{2,1,0:T(8,128)}), f32[384,8,128]{2,1,0:T(8,128)S(1)}, u32[]{:S(2)}, u32[]{:S(2)}) %all-to-all-start) | async-done | bytes 1572896 | tf_op jit(solution)/shard_map/all_to_all | solution.py:568
  38.1 7.5 %shard_map.52 = f32[3200,128]{1,0:T(8,128)S(1)} custom-call(s32[1]{0:T(128)} %bitcast.first_ref, f32[3]{0:T(128)S(1)} %pad_maximum_fusion.weight_ref, f32[3072,128]{1,0:T(8,128)S(1)} %bitcast.15, f32[256,512]{1,0:T(8,128)S(1)} %collective-permute-done.other_ref, bf16[2,256,256]{2,1,0:T(8,128)(2,1)S(1)} %get-tuple-element.15.slope_ref, ...), custom_call_target="tpu_custom_call" | custom-call | flops 8000000000 | bytes 4194304 | tf_op jit(solution)/shard_map/pallas_call | solution.py:605
  45.7 31.1 %all_to_all.10 = f32[3200,1,128]{2,1,0:T(1,128)S(1)} all-to-all(f32[3200,1,128]{2,1,0:T(1,128)S(1)} %bitcast.13), channel_id=1, replica_groups=mesh['gz_0'=4,'gz_1'=4,'gz_2'=4,'gz_3'=2] {'gz_3','gz_0','gz_1','gz_2'}, dimensions={0} | all-to-all | bytes 3276800 | tf_op jit(solution)/shard_map/all_to_all | solution.py:568
  76.8 1.9 %shard_map.53 = (f32[512,256]{1,0:T(8,128)}, f32[2]{0:T(128)}) custom-call(f32[3200,128]{1,0:T(8,128)S(1)} %bitcast.14, bf16[2,256,512]{2,1,0:T(8,128)(2,1)S(1)} %get-tuple-element.21.yb_ref, bf16[2,256,256]{2,1,0:T(8,128)(2,1)S(1)} %get-tuple-element.15.slope_ref), custom_call_target="tpu_custom_call" | custom-call | flops 1000000000 | bytes 4194304 | tf_op jit(solution)/shard_map/pallas_call | solution.py:624
Async XLA Ops:
  3.8 34.3 %all-to-all-start = ((f32[384,8,128]{2,1,0:T(8,128)}), f32[384,8,128]{2,1,0:T(8,128)S(1)}, u32[]{:S(2)}, u32[]{:S(2)}) async-start(f32[384,8,128]{2,1,0:T(8,128)} %bitcast.4), calls=%async_computation | async-start | bytes 3145728 | tf_op jit(solution)/shard_map/all_to_all | solution.py:568
  15.3 6.4 %collective-permute-start = (f32[256,512]{1,0:T(8,128)S(1)}, f32[256,512]{1,0:T(8,128)S(1)}, u32[]{:S(2)}, u32[]{:S(2)}) collective-permute-start(f32[256,512]{1,0:T(8,128)S(1)} %get-tuple-element.14), channel_id=1, source_target_pairs={{0,64}} | collective-permute-start | bytes 1572872 | tf_op jit(solution)/shard_map/ppermute | solution.py:586
  18.2 1.0 %copy-start = (bf16[2,2,256,512]{3,2,1,0:T(8,128)(2,1)}, bf16[2,2,256,512]{3,2,1,0:T(8,128)(2,1)S(1)}, u32[]{:S(2)}) copy-start(bf16[2,2,256,512]{3,2,1,0:T(8,128)(2,1)S(1)} %get-tuple-element.17.wx_hbm) | copy-start | bytes 3145732
  19.1 1.0 %copy-start.1 = (bf16[2,2,512,256]{3,2,1,0:T(8,128)(2,1)}, bf16[2,2,512,256]{3,2,1,0:T(8,128)(2,1)S(1)}, u32[]{:S(2)}) copy-start(bf16[2,2,512,256]{3,2,1,0:T(8,128)(2,1)S(1)} %get-tuple-element.20.wxi_hbm) | copy-start | bytes 3145732
  20.1 0.8 %copy-start.2 = (bf16[2,512,256]{2,1,0:T(8,128)(2,1)}, bf16[2,512,256]{2,1,0:T(8,128)(2,1)S(1)}, u32[]{:S(2)}) copy-start(bf16[2,512,256]{2,1,0:T(8,128)(2,1)S(1)} %get-tuple-element.18.wz_hbm) | copy-start | bytes 1572868
  20.9 0.7 copy-start.3
